TPU v7x, 256 devices: a whole 4x4x8 slice. The times are simulated.
256 devices in a mesh: vocab: 32 (over z, y), section: 8 (over x, core).
Axes of the slice: x: 4, y: 4, z: 8, core: 2. Of those that a mesh axis runs over, the one named last changes fastest.
Arguments:
- hidden: bfloat16 [512, 8192], P('section', 'vocab'), may hold values from -2 to 2
- targets: int32 [512], replicated, may hold values from 0 to 98303
- out_weight: bfloat16 [98304, 8192], P(('vocab', 'section')), may hold values from -2 to 2
Outputs:
- token_loss: float32 [512], replicated
- weight_grad: bfloat16 [98304, 8192], P(('vocab', 'section'))
- sent_grad: bfloat16 [512, 8192], P('section', 'vocab')
All inputs are finite; a program needn't handle non-finite values.
Results may differ from a plain program's by a relative error of at most 0.0033.
Values may be sent and summed in bfloat16 or wider, within the bound.
A program may use at most 128 MiB of HBM per device.

v0:
```python
import jax
import jax.numpy as jnp
from jax import lax
from jax.sharding import Mesh
from jax.sharding import PartitionSpec as P

VOCAB = ("vocab_0", "vocab_1")
SECTION = ("section_0", "section_1")
VOCAB_SECTION = ("vocab_0", "vocab_1", "section_0", "section_1")


def sent_to_all(value, axis):
    copies = jnp.broadcast_to(value, (lax.axis_size(axis), *value.shape))
    return lax.all_to_all(copies, axis, split_axis=0, concat_axis=0, tiled=True)


def laid_out(blocks, dim):
    blocks = jnp.moveaxis(blocks, 0, dim)
    dims = blocks.shape
    return blocks.reshape(*dims[:dim], dims[dim] * dims[dim + 1], *dims[dim + 2 :])


def gathered_copies(value, axis, dim):
    blocks = sent_to_all(value, axis)
    return laid_out(blocks, dim)


def collected_together(value, axis):
    leaves = jax.tree.leaves(value)
    sequence = sorted(range(len(leaves)), key=lambda k: -leaves[k].size)
    width = (1, *leaves[sequence[0]].shape)[-1]
    lines = [
        jnp.pad(leaves[k].reshape(-1), (0, -leaves[k].size % width)).reshape(-1, width)
        for k in sequence
    ]
    both, at, found = (lax.all_gather(jnp.concatenate(lines), axis), 0, {})
    for k, line in zip(sequence, lines):
        piece = both[:, at : at + len(line)].reshape(len(both), -1)
        found[k] = piece[:, : leaves[k].size].reshape(-1, *leaves[k].shape)
        at += len(line)
    numbers = iter(range(len(leaves)))
    return jax.tree.map(lambda _: found[next(numbers)], value)


def combined_by_axis(value, axes, combine):
    for axis in axes:
        pieces = collected_together(value, axis)
        value = jax.tree.map(lambda part: part[0], pieces)
        for k in range(1, lax.axis_size(axis)):
            value = combine(value, jax.tree.map(lambda part: part[k], pieces))
    return value


def split_up(value, dim, devices):
    before, after = (value.shape[:dim], value.shape[dim + 1 :])
    return jnp.moveaxis(value.reshape(*before, devices, -1, *after), dim, 0)


def summed_on_arrival(value, axis, dim):
    blocks = split_up(value, dim, lax.axis_size(axis))
    arrived = lax.all_to_all(blocks, axis, split_axis=0, concat_axis=0, tiled=True)
    return arrived.sum(axis=0)


def shifted(value, axis, steps):
    count = lax.axis_size(axis)
    pairs = [(source, (source + steps) % count) for source in range(count)]
    return lax.ppermute(value, axis, pairs)


def combine(first, second):
    top_a, sum_a, hit_a = first
    top_b, sum_b, hit_b = second
    top = jnp.maximum(top_a, top_b)
    return (top, sum_a * jnp.exp(top_a - top) + sum_b * jnp.exp(top_b - top), hit_a + hit_b)


def on_device(hidden, targets, out_weight):
    columns = gathered_copies(hidden, VOCAB, 1)
    whole = lax.all_gather(columns, SECTION, axis=0, tiled=True)
    rows = out_weight.shape[0]
    offset = lax.axis_index(VOCAB_SECTION) * rows
    logits = jnp.einsum("td,vd->tv", whole, out_weight, preferred_element_type=jnp.float32)
    picked = targets[:, None] - offset == jnp.arange(rows, dtype=jnp.int32)[None, :]
    local_hit = jnp.sum(jnp.where(picked, logits, jnp.float32(0.0)), axis=1)
    local_top = jnp.max(logits, axis=1)
    local_sum = jnp.sum(jnp.exp(logits - local_top[:, None]), axis=1)
    top, total, target_logit = combined_by_axis(
        (local_top, local_sum, local_hit), VOCAB_SECTION, combine
    )
    token_loss = top + jnp.log(total) - target_logit
    probs = jnp.exp(logits - top[:, None]) / total[:, None]
    dlogits = (probs - picked.astype(jnp.float32)).astype(jnp.bfloat16)
    weight_grad = jnp.einsum(
        "tv,td->vd", dlogits, whole, preferred_element_type=jnp.float32
    ).astype(jnp.bfloat16)
    token_block = lax.psum_scatter(
        jnp.dot(dlogits, out_weight, preferred_element_type=jnp.float32),
        SECTION,
        scatter_dimension=0,
        tiled=True,
    )
    owned = summed_on_arrival(token_block, VOCAB, 1)
    sent_grad = shifted(owned.astype(jnp.bfloat16), SECTION, -1)
    return (token_loss, weight_grad, sent_grad)


def solution(mesh):
    split = Mesh(mesh.devices.reshape(8, 4, 4, 2), ("vocab_0", "vocab_1", "section_0", "section_1"))
    placed = (P(SECTION, VOCAB), P(), P(VOCAB_SECTION, None))
    return jax.shard_map(
        on_device,
        mesh=split,
        in_specs=placed,
        out_specs=(P(), P(VOCAB_SECTION, None), P(SECTION, VOCAB)),
        check_vma=False,
    )
```

profile of v0, /device:TPU:1, one launch (start us, length us, event | category | flops | bytes accessed | tf_op | source)
XLA Modules:
  0.0 341.3 jit_solution(13021333229469894591)
XLA Ops:
  7.2 0.0 copy-start
  7.2 0.0 all-gather.10.cloned.1.call-start
  7.2 0.9 broadcast_in_dim.6
  8.1 38.0 %all_to_all.10 = bf16[32,64,256]{2,1,0:T(8,128)(2,1)S(1)} all-to-all(bf16[32,64,256]{2,1,0:T(8,128)(2,1)S(1)} %broadcast_in_dim.6), channel_id=1, replica_groups=mesh['vocab_0'=8,'vocab_1'=4,'section_0'=4,'section_1'=2] {'vocab_0','vo..., dimensions={0} | all-to-all | bytes 2097152 | tf_op jit(solution)/shard_map/all_to_all | solution.py:14
  46.1 1.0 copy.9
  47.2 0.0 all-gather.10.cloned.1.call-update
  47.2 0.0 reduce-scatter.2.cloned.1.call-start
  47.2 0.0 copy-done
  47.3 51.9 %all-gather.10.cloned.1.call-done = bf16[512,8192]{1,0:T(8,128)(2,1)} async-done(((bf16[64,8192]{1,0:T(8,128)(2,1)}), bf16[512,8192]{1,0:T(8,128)(2,1)}) %all-gather.10.cloned.1.call-update) | async-done | bytes 8388624 | tf_op jit(solution)/shard_map/all_gather | solution.py:80
  99.1 7.8 %fusion.60 = (f32[512]{0:T(512)S(1)}, f32[512,384]{0,1:T(8,128)S(1)}) fusion(bf16[512,8192]{1,0:T(8,128)(2,1)} %all-gather.10.cloned.1.call-done, bf16[384,8192]{1,0:T(8,128)(2,1)} %param.5), kind=kOutput, calls=%fused_computation.116 | convolution fusion | flops 3221421568 | bytes 15468544 | tf_op jit(solution)/shard_map/td,vd->tv/dot_general | solution.py:83
  107.0 0.2 exponential_reduce_fusion
  107.2 19.7 %all-gather.4 = f32[8,3,512]{2,1,0:T(4,128)S(1)} all-gather(f32[1,3,512]{2,1,0:T(4,128)S(1)} %maximum_bitcast_fusion), channel_id=2, replica_groups=mesh['vocab_0'=8,'vocab_1'=4,'section_0'=4,'section_1'=2] {'vocab_0'}, dimensions={0}, use_global_device_ids=true | all-gather | bytes 55296 | tf_op jit(solution)/shard_map/all_gather | solution.py:36
  126.9 0.1 fusion.22
  127.0 9.6 %all-gather.5 = f32[4,3,512]{2,1,0:T(4,128)S(1)} all-gather(f32[1,3,512]{2,1,0:T(4,128)S(1)} %maximum_bitcast_fusion.1), channel_id=3, replica_groups=mesh['vocab_0'=8,'vocab_1'=4,'section_0'=4,'section_1'=2] {'vocab_1'}, dimensions={0}, use_global_device_ids=true | all-gather | bytes 30720 | tf_op jit(solution)/shard_map/all_gather | solution.py:36
  136.7 9.0 %all-gather.6 = f32[4,3,512]{2,1,0:T(4,128)S(1)} all-gather(f32[1,3,512]{2,1,0:T(4,128)S(1)} %maximum_bitcast_fusion.2), channel_id=4, replica_groups=mesh['vocab_0'=8,'vocab_1'=4,'section_0'=4,'section_1'=2] {'section_0'}, dimensions={0}, use_global_device_ids=true | all-gather | bytes 30720 | tf_op jit(solution)/shard_map/all_gather | solution.py:36
  145.8 13.6 %all-gather.7 = f32[2,3,512]{2,1,0:T(4,128)S(1)} all-gather(f32[1,3,512]{2,1,0:T(4,128)S(1)} %maximum_bitcast_fusion.3), channel_id=5, replica_groups=mesh['vocab_0'=8,'vocab_1'=4,'section_0'=4,'section_1'=2] {'section_1'}, dimensions={0}, use_global_device_ids=true | all-gather | bytes 18432 | tf_op jit(solution)/shard_map/all_gather | solution.py:36
  159.4 0.6 add_subtract_fusion
  160.0 10.9 %fusion.55 = f32[512,8192]{1,0:T(8,128)} fusion(bf16[384,8192]{1,0:T(8,128)(2,1)} %param.5, f32[512,384]{0,1:T(8,128)S(1)} %get-tuple-element.20, f32[512]{0:T(512)S(1)} %get-tuple-element.6, f32[512]{0:T(512)S(1)} %get-tuple-element.7, s32[512]{0:T(512)S(1)} %broadcast_subtract_fusion), kind=kOutput, calls=%fused_computation.114 | convolution fusion | flops 3222405120 | bytes 23861248 | tf_op jit(solution)/shard_map/dot_general | solution.py:98
  170.9 0.0 reduce-scatter.2.cloned.1.call-update
  171.0 91.3 %reduce-scatter.2.cloned.1.call-done = f32[64,8192]{1,0:T(8,128)} async-done(((f32[512,8192]{1,0:T(8,128)}), f32[64,8192]{1,0:T(8,128)}) %reduce-scatter.2.cloned.1.call-update) | async-done | bytes 2097168 | tf_op jit(solution)/shard_map/reduce_scatter | solution.py:97
  262.3 1.8 copy.11
  264.1 57.7 %all_to_all.11 = f32[32,64,256]{2,1,0:T(8,128)S(1)} all-to-all(f32[32,64,256]{2,1,0:T(8,128)S(1)} %bitcast.336), channel_id=1, replica_groups=mesh['vocab_0'=8,'vocab_1'=4,'section_0'=4,'section_1'=2] {'vocab_0','vo..., dimensions={0} | all-to-all | bytes 4194304 | tf_op jit(solution)/shard_map/all_to_all | solution.py:61
  321.8 0.1 reduce_sum.29
  322.0 3.1 collective-permute-start
  325.1 8.7 %convolution_convert_fusion = bf16[384,8192]{1,0:T(8,128)(2,1)} fusion(bf16[512,8192]{1,0:T(8,128)(2,1)} %all-gather.10.cloned.1.call-done, f32[512,384]{0,1:T(8,128)S(1)} %get-tuple-element.20, f32[512]{0:T(512)S(1)} %get-tuple-element.6, f32[512]{0:T(512)S(1)} %get-tuple-element.7, s32[512]{0:T(512)S(1)} %broadcast_subtract_fusion), kind=kOutput, calls=%fused_computation | convolution fusion | flops 3225550848 | bytes 15472640 | tf_op jit(solution)/shard_map/tv,td->vd/dot_general | solution.py:94
  333.8 0.0 collective-permute-done
  333.8 0.6 copy.13
  (11 shorter events, 0.2 us)
Async XLA Ops:
  7.2 40.1 %copy-start = (s32[512]{0:T(512)S(1)}, s32[512]{0:T(512)}, u32[]{:S(2)}) copy-start(s32[512]{0:T(512)} %param.4) | copy-start | bytes 6148
  7.2 91.9 %all-gather.10.cloned.1.call-start = ((), (), s32[]{:S(2)}) async-start(), calls=%async_computation.3 | async-start | bytes 9437184 | tf_op jit(solution)/shard_map/all_gather | solution.py:80
  47.2 215.1 %reduce-scatter.2.cloned.1.call-start = ((), (), s32[]{:S(2)}) async-start(), calls=%async_computation.4 | async-start | bytes 18874368 | tf_op jit(solution)/shard_map/reduce_scatter | solution.py:97
  322.0 11.9 %collective-permute-start = (bf16[64,256]{1,0:T(8,128)(2,1)S(1)}, bf16[64,256]{1,0:T(8,128)(2,1)S(1)}, u32[]{:S(2)}, u32[]{:S(2)}) collective-permute-start(bf16[64,256]{1,0:T(8,128)(2,1)S(1)} %reduce_sum.29), channel_id=1, source_target_pairs={{0,7},{1,0},{2,1},{3,2},{4,3},{5,4},{6,5},{7,6},{8,15},{9,8},{10,9... | collective-permute-start | bytes 98312 | tf_op jit(solution)/shard_map/ppermute | solution.py:68
Sparse Core Ops, SparseCore 0:
  47.3 51.7 all-gather.9
  171.1 91.1 reduce-scatter.1
where the time goes:
time: 342 us; the launch traced here: 341 us
  blocking collectives  148 us (43%)
  waiting for transfers between devices  143 us (42%)
  matrix products  27.5 us (8%)
  between operations  14.2 us (4%)
  local copies, waits for them, and re-layouts  4.34 us (1%)
    reduce_scatter x1, waiting for transfers between devices, on_device(): lax.psum_scatter(jnp.dot(dlogits, out_weight, preferred_element_type=jnp....  91.3 us
    all_to_all x1, blocking collectives, summed_on_arrival(): lax.all_to_all(blocks, axis, split_axis=0, concat_axis=0, tiled=True)  57.7 us
    all_gather x4, blocking collectives, collected_together(): both, at, found = (lax.all_gather(jnp.concatenate(lines), axis), 0, {})  52 us
    all_gather x1, waiting for transfers between devices, on_device(): whole = lax.all_gather(columns, SECTION, axis=0, tiled=True)  51.9 us
    all_to_all x1, blocking collectives, sent_to_all(): return lax.all_to_all(copies, axis, split_axis=0, concat_axis=0, tiled=True)  38 us
    dot_general x1, matrix products, on_device(): jnp.dot(dlogits, out_weight, preferred_element_type=jnp.float32)  10.9 us
    dot_general x1, matrix products, on_device(): jnp.einsum('tv,td->vd', dlogits, whole, preferred_element_type=jnp.float32)  8.73 us
    dot_general x1, matrix products, on_device(): jnp.einsum('td,vd->tv', whole, out_weight, preferred_element_type=jnp.flo...  7.84 us
  transfers between devices with their start and end apart: 3, of which 2 were waited for; matrix products, arithmetic and copies ran while one was open for 3% of the time, Pallas kernels for 0%

commit v1 on v0

v1 whole, which is shorter than its diff:
```python
import jax
import jax.numpy as jnp
from jax import lax
from jax.experimental import pallas as pl
from jax.experimental.pallas import tpu as pltpu
from jax.sharding import PartitionSpec as P

NZ, NY, NX, NC = 8, 4, 4, 2
D, T, RV = 8192, 512, 384
BC = 48
MESH = pl.DeviceIdType.MESH
F32, BF16 = jnp.float32, jnp.bfloat16
N_SEM = 160


def packed(row):
    return jnp.concatenate([row[:, 128 * k : 128 * (k + 1)] for k in range(4)], axis=0)


def unpacked(block):
    return jnp.concatenate([block[k : k + 1, :] for k in range(4)], axis=1)


def body(hid, tgt, w, loss, wg, dl_out, gat, wv, wo, acc, dlt, stage, rx_c, rx_p, rx_z,
         send_sem, recv_sem, load_sem, own_sem, out_sem):
    v, s = lax.axis_index("vocab"), lax.axis_index("section")
    z, y, x, c = v // NY, lax.rem(v, NY), s // NC, lax.rem(s, NC)
    o = 1 - c

    def dev(z_, y_, x_, c_):
        return (z_ * NY + y_, x_ * NC + c_)

    def zz(k):
        return lax.rem(z + (k + NZ), NZ)

    def yy(k):
        return lax.rem(y + (k + NY), NY)

    def xx(k):
        return lax.rem(x + (k + NX), NX)

    def load_w(k, _):
        own = pltpu.make_async_copy(
            w.at[:, pl.ds(pl.multiple_of(k * 256 + c * 128, 128), 128)], wv.at[k], load_sem.at[0]
        )
        other = pltpu.make_async_copy(
            w.at[:, pl.ds(pl.multiple_of(k * 256 + o * 128, 128), 128)], wo.at[k], load_sem.at[1]
        )
        own.start()
        other.start()
        return 0

    mine = [
        pltpu.make_async_copy(
            hid.at[:, pl.ds(128 * h, 128)], gat.at[h, z, y, x, c], own_sem.at[h]
        )
        for h in range(2)
    ]
    for copy in mine:
        copy.start()
    lax.fori_loop(0, NZ * NY, load_w, 0)

    plane = [(i, j) for i in range(NX) for j in range(NY) if (i, j) != (0, 0)]
    barrier = pltpu.get_barrier_semaphore()
    pl.semaphore_signal(barrier, inc=1, device_id=dev(z, y, x, o), device_id_type=MESH)
    for i, j in plane:
        pl.semaphore_signal(barrier, inc=1, device_id=dev(z, yy(j), xx(i), c), device_id_type=MESH)
    for k in range(1, NZ):
        pl.semaphore_signal(barrier, inc=1, device_id=dev(zz(k), y, x, c), device_id_type=MESH)
    pl.semaphore_wait(barrier, 1 + len(plane) + NZ - 1)
    for copy in mine:
        copy.wait()

    count = [0]
    sends = []

    def slot():
        count[0] += 1
        return count[0] - 1

    def send(ref, device, k):
        copy = pltpu.make_async_remote_copy(
            src_ref=ref, dst_ref=ref, send_sem=send_sem.at[k], recv_sem=recv_sem.at[k],
            device_id=device, device_id_type=MESH,
        )
        copy.start()
        sends.append(copy)

    def arrived(ref, k):
        pltpu.make_async_remote_copy(
            src_ref=ref, dst_ref=ref, send_sem=send_sem.at[k], recv_sem=recv_sem.at[k],
            device_id=dev(z, y, x, o), device_id_type=MESH,
        ).wait_recv()

    passed = []

    def pass_on(view):
        k = slot()
        send(view(c), dev(z, y, x, o), k)
        passed.append((view, k))

    first_z, first_p = [slot() for _ in range(1, NZ)], [slot() for _ in plane]
    for k in range(1, NZ):
        send(gat.at[:, z, y, x, c, 0:BC, :], dev(zz(k), y, x, c), first_z[k - 1])
    for (i, j), k in zip(plane, first_p):
        send(gat.at[:, z, y, x, c, BC:64, :], dev(z, yy(j), xx(i), c), k)

    def b_view(y_, x_, lo, hi):
        return lambda core: gat.at[0, lo:hi, y_, x_, core, 0:BC, :]

    def c_view(y_, x_, lo, hi):
        return lambda core: gat.at[1, lo:hi, y_, x_, core, 0:BC, :]

    def a_view(h, z_):
        return lambda core: gat.at[h, z_, :, :, core, BC:64, :]

    class Ring:
        def __init__(self, view, along):
            self.view, self.along = view, along
            self.k = [slot() for _ in range(4)]

        def to(self, step):
            return dev(z, y, xx(step), c) if self.along == "x" else dev(z, yy(step), x, c)

        def open(self):
            send(self.view(0, 0, NZ)(c), self.to(1), self.k[0])
            send(self.view(0, 0, NZ)(c), self.to(-1), self.k[1])

        def middle(self):
            low, high = self.view(-1, 0, NZ), self.view(1, 0, NZ)
            arrived(low(c), self.k[0])
            send(self.view(-1, 0, 4)(c), self.to(1), self.k[2])
            pass_on(low)
            arrived(high(c), self.k[1])
            send(self.view(1, 4, NZ)(c), self.to(-1), self.k[3])
            pass_on(high)

        def close(self):
            low, high = self.view(-2, 0, 4), self.view(2, 4, NZ)
            arrived(low(c), self.k[2])
            pass_on(low)
            arrived(high(c), self.k[3])
            pass_on(high)

    b_y = Ring(lambda step, lo, hi: b_view(yy(step), x, lo, hi), "y")
    c_x = Ring(lambda step, lo, hi: c_view(y, xx(step), lo, hi), "x")
    b_x = [Ring(lambda step, lo, hi, j=j: b_view(yy(j), xx(step), lo, hi), "x") for j in (0, -1, 1, 2)]
    c_y = [Ring(lambda step, lo, hi, i=i: c_view(yy(step), xx(i), lo, hi), "y") for i in (0, -1, 1, 2)]
    a_up = [[slot() for _ in range(2)] for _ in range(3)] + [[slot()]]
    a_down = [[slot() for _ in range(2)] for _ in range(3)] + [[slot()]]

    for k in range(1, NZ):
        arrived(gat.at[:, zz(-k), y, x, c, 0:BC, :], first_z[k - 1])
    b_y.open()
    c_x.open()
    b_x[0].open()
    c_y[0].open()
    pass_on(lambda core: gat.at[:, :, y, x, core, 0:BC, :])
    for (i, j), k in zip(plane, first_p):
        arrived(gat.at[:, z, yy(-j), xx(-i), c, BC:64, :], k)
    for h in range(2):
        send(a_view(h, z)(c), dev(zz(1), y, x, c), a_up[0][h])
        send(a_view(h, z)(c), dev(zz(-1), y, x, c), a_down[0][h])
    pass_on(lambda core: gat.at[:, z, :, :, core, BC:64, :])

    def a_step(step):
        for h in range(2):
            if h < len(a_up[step - 1]):
                view = a_view(h, zz(-step))
                arrived(view(c), a_up[step - 1][h])
                if step < 3 or (step == 3 and h == 0):
                    send(view(c), dev(zz(1), y, x, c), a_up[step][h])
                pass_on(view)
            lower = h if step < 4 else 1 - h
            if h < len(a_down[step - 1]):
                view = a_view(lower, zz(step))
                arrived(view(c), a_down[step - 1][h])
                if step < 3:
                    send(view(c), dev(zz(-1), y, x, c), a_down[step][h])
                elif step == 3 and h == 1:
                    send(view(c), dev(zz(-1), y, x, c), a_down[step][0])
                pass_on(view)

    b_y.middle()
    b_x[1].open()
    b_x[2].open()
    c_x.middle()
    c_y[1].open()
    c_y[2].open()
    a_step(1)
    b_x[0].middle()
    c_y[0].middle()
    b_y.close()
    b_x[3].open()
    c_x.close()
    c_y[3].open()
    a_step(2)
    b_x[1].middle()
    c_y[1].middle()
    b_x[0].close()
    c_y[0].close()
    b_x[2].middle()
    c_y[2].middle()
    a_step(3)
    b_x[1].close()
    c_y[1].close()
    b_x[3].middle()
    c_y[3].middle()
    b_x[2].close()
    c_y[2].close()
    a_step(4)
    b_x[3].close()
    c_y[3].close()
    for view, k in list(passed):
        arrived(view(o), k)
    pltpu.make_async_copy(wo, wv, load_sem.at[0]).wait()
    pltpu.make_async_copy(wv, wo, load_sem.at[1]).wait()

    acc[...] = jnp.zeros_like(acc)

    def logits_step(k, _):
        left, right = [], []
        for j in range(NY):
            left += [wv[k * NY + j], wo[k * NY + j]]
            right += [gat[c, k, j].reshape(T, 128), gat[o, k, j].reshape(T, 128)]
        acc[...] += lax.dot_general(
            jnp.concatenate(left, axis=1), jnp.concatenate(right, axis=1),
            (((1,), (1,)), ((), ())), preferred_element_type=F32,
        )
        return 0

    lax.fori_loop(0, NZ, logits_step, 0)

    offset = (v * (NX * NC) + s) * RV
    picked = tgt[...] - offset == lax.broadcasted_iota(jnp.int32, (RV, T), 0)
    logits = acc[...]
    hit = jnp.sum(jnp.where(picked, logits, 0.0), axis=0, keepdims=True)
    top = jnp.max(logits, axis=0, keepdims=True)
    total = jnp.sum(jnp.exp(logits - top), axis=0, keepdims=True)
    state = jnp.concatenate([packed(top), packed(total), packed(hit), jnp.zeros((4, 128), F32)], axis=0)

    def merged(blocks):
        tops = [block[0:4] for block in blocks]
        top = tops[0]
        for one in tops[1:]:
            top = jnp.maximum(top, one)
        total, hit = jnp.zeros_like(top), jnp.zeros_like(top)
        for block, one in zip(blocks, tops):
            total = total + block[4:8] * jnp.exp(one - top)
            hit = hit + block[8:12]
        return jnp.concatenate([top, total, hit, jnp.zeros((4, 128), F32)], axis=0)

    def exchanged(state, buf, me, n, peers):
        buf[me] = state
        todo = []
        for device, source, k in peers:
            send(buf.at[me], device, k)
            todo.append((source, k))
        for source, k in todo:
            arrived(buf.at[source], k)
        return merged([buf[k] for k in range(n)])

    state = exchanged(state, rx_c, c, 2, [(dev(z, y, x, o), o, slot())])
    state = exchanged(
        state, rx_p, x * NY + y, NX * NY,
        [(dev(z, yy(j), xx(i), c), xx(-i) * NY + yy(-j), slot()) for i, j in plane],
    )
    state = exchanged(
        state, rx_z, z, NZ, [(dev(zz(k), y, x, c), zz(-k), slot()) for k in range(1, NZ)]
    )
    loss[...] = state[0:4] + jnp.log(state[4:8]) - state[8:12]
    top, total = unpacked(state[0:4]), unpacked(state[4:8])
    dlt[...] = (jnp.exp(acc[...] - top) / total - picked.astype(F32)).astype(BF16)

    for k in range(NZ):
        right = []
        for j in range(NY):
            right += [gat[0, k, j].reshape(T, 128), gat[1, k, j].reshape(T, 128)]
        stage[k] = jnp.dot(
            dlt[...], jnp.concatenate(right, axis=1), preferred_element_type=F32
        ).astype(BF16)
        pltpu.make_async_copy(stage.at[k], wg.at[:, pl.ds(k * 1024, 1024)], out_sem.at[k]).start()
    dl_out[...] = dlt[...]
    for k in range(NZ):
        pltpu.make_async_copy(stage.at[k], wg.at[:, pl.ds(k * 1024, 1024)], out_sem.at[k]).wait()
    for copy in sends:
        copy.wait_send()
    assert count[0] <= N_SEM, count


def forward(hidden, targets, out_weight):
    hbm, vmem = pl.BlockSpec(memory_space=pl.ANY), pl.BlockSpec(memory_space=pltpu.VMEM)
    loss, wg, dlt = pl.pallas_call(
        body,
        out_shape=(
            jax.ShapeDtypeStruct((4, 128), F32),
            jax.ShapeDtypeStruct((RV, D), BF16),
            jax.ShapeDtypeStruct((RV, T), BF16),
        ),
        in_specs=[hbm, vmem, hbm],
        out_specs=(vmem, hbm, vmem),
        scratch_shapes=[
            pltpu.VMEM((2, NZ, NY, NX, NC, 64, 128), BF16),
            pltpu.VMEM((NZ * NY, RV, 128), BF16),
            pltpu.VMEM((NZ * NY, RV, 128), BF16),
            pltpu.VMEM((RV, T), F32),
            pltpu.VMEM((RV, T), BF16),
            pltpu.VMEM((NZ, RV, 1024), BF16),
            pltpu.VMEM((NC, 16, 128), F32),
            pltpu.VMEM((NX * NY, 16, 128), F32),
            pltpu.VMEM((NZ, 16, 128), F32),
            pltpu.SemaphoreType.DMA((N_SEM,)),
            pltpu.SemaphoreType.DMA((N_SEM,)),
            pltpu.SemaphoreType.DMA((2,)),
            pltpu.SemaphoreType.DMA((2,)),
            pltpu.SemaphoreType.DMA((NZ,)),
        ],
        compiler_params=pltpu.CompilerParams(
            collective_id=0, has_side_effects=True, vmem_limit_bytes=60 * 2**20
        ),
    )(hidden, targets.reshape(1, T), out_weight)
    return loss.reshape(T), wg, dlt


def on_device(hidden, targets, out_weight):
    token_loss, weight_grad, dlt = forward(hidden, targets, out_weight)
    partial = lax.dot_general(
        dlt, out_weight, (((0,), (0,)), ((), ())), preferred_element_type=F32
    )
    block = lax.psum_scatter(partial, "section", scatter_dimension=0, tiled=True)
    pieces = jnp.moveaxis(block.reshape(64, NZ * NY, 256), 1, 0)
    owned = lax.all_to_all(pieces, "vocab", split_axis=0, concat_axis=0, tiled=True).sum(axis=0)
    n = NX * NC
    sent = lax.ppermute(owned.astype(BF16), "section", [(k, (k - 1) % n) for k in range(n)])
    return token_loss, weight_grad, sent


def solution(mesh):
    placed = (P("section", "vocab"), P(), P(("vocab", "section"), None))
    return jax.shard_map(
        on_device, mesh=mesh, in_specs=placed,
        out_specs=(P(), P(("vocab", "section"), None), P("section", "vocab")),
        check_vma=False,
    )
```

time: 342 us -> 257 us (0.75)
  blocking collectives: 148 us -> 57.8 us
  Pallas kernels: 0 us -> 63.4 us
  waiting for transfers between devices: 143 us -> 95.4 us
  matrix products: 27.5 us -> 13.2 us
  local copies, waits for them, and re-layouts: 4.34 us -> 9.21 us
    pallas_call x0 -> x1, Pallas kernels: none -> 63.4 us  [forward(): pl.pallas_call(body, out_shape=(jax.ShapeDtypeStruct((4, 128), F32), jax....]
    all_gather x4 -> x0, blocking collectives: 52 us -> none  [collected_together(): both, at, found = (lax.all_gather(jnp.concatenate(lines), axis), 0, {})]
    all_gather x1 -> x0, waiting for transfers between devices: 51.9 us -> none  [on_device(): whole = lax.all_gather(columns, SECTION, axis=0, tiled=True)]
    all_to_all x2 -> x1, blocking collectives: 95.7 us -> 57.8 us  [on_device(): lax.all_to_all(pieces, 'vocab', split_axis=0, concat_axis=0, tiled=True)]
    dot_general x3 -> x1, matrix products: 27.5 us -> 13.2 us  [on_device(): lax.dot_general(dlt, out_weight, (((0,), (0,)), ((), ())), preferred_elem...]
    unnamed x3 -> x5, local copies, waits for them, and re-layouts: 0.62 us -> 7.39 us
  transfers between devices with their start and end apart: 3 -> 2, of which waited for: 2 -> 2; matrix products, arithmetic and copies ran while one was open for 3% -> 0% of each run, Pallas kernels for 0% -> 0%
where the time goes in v1:
time: 257 us; the launch traced here: 256 us
  waiting for transfers between devices  95.4 us (37%)
  Pallas kernels  63.4 us (25%)
  blocking collectives  57.8 us (22%)
  between operations  14.1 us (5%)
  matrix products  13.2 us (5%)
  local copies, waits for them, and re-layouts  9.21 us (4%)
  starting transfers between devices  3.16 us (1%)
    reduce_scatter x1, waiting for transfers between devices, on_device(): lax.psum_scatter(partial, 'section', scatter_dimension=0, tiled=True)  93.2 us
    pallas_call x1, Pallas kernels, forward(): pl.pallas_call(body, out_shape=(jax.ShapeDtypeStruct((4, 128), F32), jax....  63.4 us
    all_to_all x1, blocking collectives, on_device(): lax.all_to_all(pieces, 'vocab', split_axis=0, concat_axis=0, tiled=True)  57.8 us
    dot_general x1, matrix products, on_device(): lax.dot_general(dlt, out_weight, (((0,), (0,)), ((), ())), preferred_elem...  13.2 us
    unnamed x5, local copies, waits for them, and re-layouts  7.39 us
  transfers between devices with their start and end apart: 2, of which 2 were waited for; matrix products, arithmetic and copies ran while one was open for 0% of the time, Pallas kernels for 0%

profile of v1, /device:TPU:1, one launch (start us, length us, event | category | flops | bytes accessed | tf_op | source)
XLA Modules:
  0.0 256.4 jit_solution(1842642773703335318)
XLA Ops:
  7.2 0.0 reduce-scatter.2.cloned.1.call-start
  7.2 63.4 %shard_map.58 = (f32[4,128]{1,0:T(4,128)}, bf16[384,8192]{1,0:T(8,128)(2,1)}, bf16[384,512]{1,0:T(8,128)(2,1)}) custom-call(bf16[64,256]{1,0:T(8,128)(2,1)} %hid.1, s32[1,512]{1,0:T(1,128)} %bitcast.13, bf16[384,8192]{1,0:T(8,128)(2,1)} %w.1), custom_call_target="tpu_custom_call" | custom-call | tf_op jit(solution)/shard_map/pallas_call | solution.py:293
  70.7 13.2 %fusion = f32[512,8192]{1,0:T(8,128)} fusion(bf16[384,512]{1,0:T(8,128)(2,1)} %get-tuple-element.8, bf16[384,8192]{1,0:T(8,128)(2,1)} %w.1), kind=kOutput, calls=%fused_computation.1 | convolution fusion | flops 3221225472 | bytes 23461888 | tf_op jit(solution)/shard_map/dot_general | solution.py:327
  83.9 0.0 reduce-scatter.2.cloned.1.call-update
  83.9 0.0 copy-start
  83.9 93.2 %reduce-scatter.2.cloned.1.call-done = f32[64,8192]{1,0:T(8,128)} async-done(((f32[512,8192]{1,0:T(8,128)}), f32[64,8192]{1,0:T(8,128)}) %reduce-scatter.2.cloned.1.call-update) | async-done | bytes 2097168 | tf_op jit(solution)/shard_map/reduce_scatter | solution.py:330
  177.1 1.8 copy.9
  178.9 57.8 %all_to_all.5 = f32[32,64,256]{2,1,0:T(8,128)S(1)} all-to-all(f32[32,64,256]{2,1,0:T(8,128)S(1)} %bitcast.11), channel_id=1, replica_groups=mesh['vocab'=32,'section'=8] {'vocab'}, dimensions={0} | all-to-all | bytes 4194304 | tf_op jit(solution)/shard_map/all_to_all | solution.py:332
  236.7 0.1 reduce_sum.9
  236.8 3.1 %collective-permute-start = (bf16[64,256]{1,0:T(8,128)(2,1)S(1)}, bf16[64,256]{1,0:T(8,128)(2,1)S(1)}, u32[]{:S(2)}, u32[]{:S(2)}) collective-permute-start(bf16[64,256]{1,0:T(8,128)(2,1)S(1)} %reduce_sum.9), channel_id=1, source_target_pairs={{0,7},{1,0},{2,1},{3,2},{4,3},{5,4},{6,5},{7,6},{8,15},{9,8},{10,9... | collective-permute-start | bytes 98312 | tf_op jit(solution)/shard_map/ppermute | solution.py:334
  239.9 2.2 collective-permute-done
  242.1 0.0 copy-done
  242.1 0.6 copy.13
  242.7 6.2 %copy.14 = bf16[384,8192]{1,0:T(8,128)(2,1)} copy(bf16[384,8192]{1,0:T(8,128)(2,1)} %get-tuple-element.13) | data formatting | bytes 12582912
  248.9 0.6 copy.15
Async XLA Ops:
  7.2 169.9 %reduce-scatter.2.cloned.1.call-start = ((), (), s32[]{:S(2)}) async-start(), calls=%async_computation.2 | async-start | bytes 18874368 | tf_op jit(solution)/shard_map/reduce_scatter | solution.py:330
  83.9 158.3 %copy-start = (f32[4,128]{1,0:T(4,128)S(1)}, f32[4,128]{1,0:T(4,128)}, u32[]{:S(2)}) copy-start(f32[4,128]{1,0:T(4,128)} %get-tuple-element.6) | copy-start | bytes 6148
  236.8 5.3 %collective-permute-start = (bf16[64,256]{1,0:T(8,128)(2,1)S(1)}, bf16[64,256]{1,0:T(8,128)(2,1)S(1)}, u32[]{:S(2)}, u32[]{:S(2)}) collective-permute-start(bf16[64,256]{1,0:T(8,128)(2,1)S(1)} %reduce_sum.9), channel_id=1, source_target_pairs={{0,7},{1,0},{2,1},{3,2},{4,3},{5,4},{6,5},{7,6},{8,15},{9,8},{10,9... | collective-permute-start | bytes 98312 | tf_op jit(solution)/shard_map/ppermute | solution.py:334
Sparse Core Ops, SparseCore 0:
  84.0 93.0 reduce-scatter.1

commit v2 on v1

--- a/solution.py
+++ b/solution.py
@@ -10,7 +10,10 @@
 BC = 48
 MESH = pl.DeviceIdType.MESH
 F32, BF16 = jnp.float32, jnp.bfloat16
-N_SEM = 160
+N_SEM = 320
+WIRE = BF16
+A, B, C = slice(0, 32), slice(32, 80), slice(80, 128)
+ORDER = (4, 3, -3, 2, -2, 1, -1, 0)
 
 
 def packed(row):
@@ -21,7 +24,8 @@
     return jnp.concatenate([block[k : k + 1, :] for k in range(4)], axis=1)
 
 
-def body(hid, tgt, w, loss, wg, dl_out, gat, wv, wo, acc, dlt, stage, rx_c, rx_p, rx_z,
+def body(hid, tgt, w, loss, wg, sent, gat, wv, wo, acc, dlt, stage, rx_c, rx_p, rx_z, dl, part,
+         sb1, rb1, sb2, rb2, sc1, rc1, sc2, rc2, sau, rau, sad, rad, ry1, ry2, rx1, rx2, rz, fa, rp, fin,
          send_sem, recv_sem, load_sem, own_sem, out_sem):
     v, s = lax.axis_index("vocab"), lax.axis_index("section")
     z, y, x, c = v // NY, lax.rem(v, NY), s // NC, lax.rem(s, NC)
@@ -41,7 +45,7 @@
 
     def load_w(k, _):
         own = pltpu.make_async_copy(
-            w.at[:, pl.ds(pl.multiple_of(k * 256 + c * 128, 128), 128)], wv.at[k], load_sem.at[0]
+            w.at[:, pl.ds(pl.multiple_of(k * 256 + c * 128, 128), 128)], wv.at[k, 0:RV], load_sem.at[0]
         )
         other = pltpu.make_async_copy(
             w.at[:, pl.ds(pl.multiple_of(k * 256 + o * 128, 128), 128)], wo.at[k], load_sem.at[1]
@@ -78,9 +82,9 @@
         count[0] += 1
         return count[0] - 1
 
-    def send(ref, device, k):
+    def send(ref, device, k, to=None):
         copy = pltpu.make_async_remote_copy(
-            src_ref=ref, dst_ref=ref, send_sem=send_sem.at[k], recv_sem=recv_sem.at[k],
+            src_ref=ref, dst_ref=ref if to is None else to, send_sem=send_sem.at[k], recv_sem=recv_sem.at[k],
             device_id=device, device_id_type=MESH,
         )
         copy.start()
@@ -104,6 +108,10 @@
         send(gat.at[:, z, y, x, c, 0:BC, :], dev(zz(k), y, x, c), first_z[k - 1])
     for (i, j), k in zip(plane, first_p):
         send(gat.at[:, z, y, x, c, BC:64, :], dev(z, yy(j), xx(i), c), k)
+
+    w_slot = slot()
+    pltpu.make_async_copy(wv.at[:, 0:RV, :], wo, load_sem.at[1]).wait()
+    send(wo, dev(z, y, x, o), w_slot, wv.at[:, RV : 2 * RV, :])
 
     def b_view(y_, x_, lo, hi):
         return lambda core: gat.at[0, lo:hi, y_, x_, core, 0:BC, :]
@@ -213,15 +221,15 @@
     c_y[3].close()
     for view, k in list(passed):
         arrived(view(o), k)
-    pltpu.make_async_copy(wo, wv, load_sem.at[0]).wait()
-    pltpu.make_async_copy(wv, wo, load_sem.at[1]).wait()
+    arrived(wv.at[:, RV : 2 * RV, :], w_slot)
+    pltpu.make_async_copy(wo, wv.at[:, 0:RV, :], load_sem.at[0]).wait()
 
     acc[...] = jnp.zeros_like(acc)
 
     def logits_step(k, _):
         left, right = [], []
         for j in range(NY):
-            left += [wv[k * NY + j], wo[k * NY + j]]
+            left += [wv[k * NY + j, 0:RV], wo[k * NY + j]]
             right += [gat[c, k, j].reshape(T, 128), gat[o, k, j].reshape(T, 128)]
         acc[...] += lax.dot_general(
             jnp.concatenate(left, axis=1), jnp.concatenate(right, axis=1),
@@ -272,7 +280,12 @@
     top, total = unpacked(state[0:4]), unpacked(state[4:8])
     dlt[...] = (jnp.exp(acc[...] - top) / total - picked.astype(F32)).astype(BF16)
 
-    for k in range(NZ):
+    own = jnp.transpose(dlt[...])
+    dl[:, 0:RV] = jnp.concatenate([own[64:T], own[0:64]], axis=0)
+    dl_slot = slot()
+    send(dl.at[:, 0:RV], dev(z, y, x, o), dl_slot, dl.at[:, RV : 2 * RV])
+
+    def weight_step(k):
         right = []
         for j in range(NY):
             right += [gat[0, k, j].reshape(T, 128), gat[1, k, j].reshape(T, 128)]
@@ -280,7 +293,195 @@
             dlt[...], jnp.concatenate(right, axis=1), preferred_element_type=F32
         ).astype(BF16)
         pltpu.make_async_copy(stage.at[k], wg.at[:, pl.ds(k * 1024, 1024)], out_sem.at[k]).start()
-    dl_out[...] = dlt[...]
+
+    def hidden_step(i):
+        zd = zz(ORDER[i])
+        right = jnp.concatenate([wv[zd * NY + j] for j in range(NY)], axis=1)
+        res = jnp.dot(dl[...], right, preferred_element_type=F32)
+        for j in range(NY):
+            part[i, j] = res[:, 128 * j : 128 * (j + 1)].reshape(NX, 128, 128)
+
+    class Heavy:
+        def __init__(self, unit, along, s1, r1, s2, r2):
+            self.unit, self.along = unit, along
+            self.s1, self.r1, self.s2, self.r2 = s1, r1, s2, r2
+            self.k = [[slot() for _ in range(4)] for _ in range(NZ)]
+
+        def to(self, step):
+            return dev(z, y, xx(step), c) if self.along == "x" else dev(z, yy(step), x, c)
+
+        def first(self, i):
+            self.s1[i] = self.unit(i, 2).astype(WIRE)
+            k = self.k[i]
+            send(self.s1.at[i, 0:2], self.to(1), k[0], self.r1.at[i, 0:2])
+            send(self.s1.at[i, 2:4], self.to(-1), k[1], self.r1.at[i, 2:4])
+
+        def second(self, i):
+            k = self.k[i]
+            for d, lo, hi in ((0, 0, 2), (1, 2, 4)):
+                step = 1 - 2 * d
+                arrived(self.r1.at[i, lo:hi], k[d])
+                mine = self.unit(i, step)
+                self.s2[i, d] = mine.astype(WIRE)
+                self.s2[i, d, lo:hi] = (mine[lo:hi] + self.r1[i, lo:hi].astype(F32)).astype(WIRE)
+                send(self.s2.at[i, d], self.to(step), k[2 + d], self.r2.at[i, d])
+
+        def third(self, i):
+            for d in range(2):
+                arrived(self.r2.at[i, d], self.k[i][2 + d])
+            return self.unit(i, 0) + self.r2[i, 0].astype(F32) + self.r2[i, 1].astype(F32)
+
+    hb = Heavy(lambda i, step: part[i, :, xx(step), B, :], "x", sb1, rb1, sb2, rb2)
+    hc = Heavy(lambda i, step: part[i, yy(step), :, C, :], "y", sc1, rc1, sc2, rc2)
+
+    def thirds(i):
+        part[i, :, x, B, :] = hb.third(i)
+        part[i, y, :, C, :] = hc.third(i)
+
+    class Light:
+        def __init__(self, at, along, r1, r2):
+            self.at, self.along, self.r1, self.r2 = at, along, r1, r2
+            self.k = [[slot() for _ in range(4)] for _ in range(2)]
+
+        def to(self, step):
+            return dev(z, y, xx(step), c) if self.along == "x" else dev(z, yy(step), x, c)
+
+        def first(self, g):
+            lo, k = 4 * g, self.k[g]
+            send(part.at[lo : lo + 2, *self.at(2)], self.to(1), k[0], self.r1.at[g, 0:2])
+            send(part.at[lo + 2 : lo + 4, *self.at(2)], self.to(-1), k[1], self.r1.at[g, 2:4])
+
+        def second(self, g):
+            lo, k = 4 * g, self.k[g]
+            for d in range(2):
+                step, h = 1 - 2 * d, 2 * d
+                arrived(self.r1.at[g, h : h + 2], k[d])
+                where = (slice(lo + h, lo + h + 2), *self.at(step))
+                part[where] = part[where] + self.r1[g, h : h + 2]
+                send(part.at[lo : lo + 4, *self.at(step)], self.to(step), k[2 + d], self.r2.at[g, d])
+
+        def third(self, g):
+            for d in range(2):
+                arrived(self.r2.at[g, d], self.k[g][2 + d])
+            where = (slice(4 * g, 4 * g + 4), *self.at(0))
+            part[where] = part[where] + self.r2[g, 0] + self.r2[g, 1]
+
+    lb = Light(lambda step: (yy(step), x, B), "y", ry1, ry2)
+    lc = Light(lambda step: (y, xx(step), C), "x", rx1, rx2)
+
+    k_up = {(off, h): slot() for off in (4, 3, 2, 1) for h in range(2)}
+    k_down = {(off, h): slot() for off in (4, 3, 2, 1) for h in range(2)}
+
+    def a_send(up, off, h):
+        i = ORDER.index(off if up or off == 4 else -off)
+        src, dst, ks, step = (sau, rau, k_up, 1) if up else (sad, rad, k_down, -1)
+        rows = slice(2 * h, 2 * h + 2)
+        value = part[i, rows, :, A, :]
+        if off < 3 or (off == 3 and h == (0 if up else 1)):
+            arrived(dst.at[off, rows], ks[off + 1, h])
+            value = value + dst[off, rows].astype(F32)
+        src[off - 1, rows] = value.astype(WIRE)
+        send(src.at[off - 1, rows], dev(zz(step), y, x, c), ks[off, h], dst.at[off - 1, rows])
+
+    k_plane = [slot() for _ in plane]
+    k_z = [slot() for _ in range(NZ - 1)]
+
+    def a_plane():
+        for h in range(2):
+            arrived(rau.at[0, 2 * h : 2 * h + 2], k_up[1, h])
+            arrived(rad.at[0, 2 * h : 2 * h + 2], k_down[1, h])
+        fa[...] = part[NZ - 1, :, :, A, :] + rau[0].astype(F32) + rad[0].astype(F32)
+        for q, (i, j) in enumerate(plane):
+            send(fa.at[yy(j), xx(i)], dev(z, yy(j), xx(i), c), k_plane[q], rp.at[q])
+
+    def z_send(i):
+        send(part.at[i, y, x, 32:128, :], dev(zz(ORDER[i]), y, x, c), k_z[i], rz.at[i])
+
+    weight_step(0)
+    weight_step(1)
+    arrived(dl.at[:, RV : 2 * RV], dl_slot)
+    for i in range(NZ):
+        hidden_step(i)
+        if i == 0:
+            a_send(True, 4, 0)
+            a_send(False, 4, 1)
+        hb.first(i)
+        hc.first(i)
+        if i == 1:
+            a_send(True, 3, 1)
+        if i == 2:
+            a_send(False, 3, 0)
+        if i == 4:
+            a_send(True, 3, 0)
+            a_send(False, 3, 1)
+        if i >= 4:
+            hb.second(i - 4)
+            hc.second(i - 4)
+        if i == 6:
+            for h in range(2):
+                a_send(True, 2, h)
+                a_send(False, 2, h)
+    hb.second(4)
+    hc.second(4)
+    weight_step(2)
+    for h in range(2):
+        a_send(True, 1, h)
+        a_send(False, 1, h)
+    hb.second(5)
+    hc.second(5)
+    weight_step(3)
+    for i in range(4):
+        thirds(i)
+    lb.first(0)
+    lc.first(0)
+    hb.second(6)
+    hc.second(6)
+    hb.second(7)
+    hc.second(7)
+    weight_step(4)
+    a_plane()
+    lb.second(0)
+    lc.second(0)
+    weight_step(5)
+    for i in range(4, 8):
+        thirds(i)
+    lb.first(1)
+    lc.first(1)
+    weight_step(6)
+    lb.third(0)
+    lc.third(0)
+    for i in range(4):
+        z_send(i)
+    weight_step(7)
+    lb.second(1)
+    lc.second(1)
+    for q in range(len(plane)):
+        arrived(rp.at[q], k_plane[q])
+    a_rows = fa[y, x]
+    for q in range(len(plane)):
+        a_rows = a_rows + rp[q]
+    fa[y, x] = a_rows
+    lb.third(1)
+    lc.third(1)
+    for i in range(4, 7):
+        z_send(i)
+    bc_rows = part[NZ - 1, y, x, 32:128, :]
+    for i in range(NZ - 1):
+        arrived(rz.at[i], k_z[i])
+        bc_rows = bc_rows + rz[i]
+    rows = jnp.concatenate([fa[y, x], bc_rows], axis=0).astype(BF16)
+    fin_slot = slot()
+    fin[0, 0] = rows[0:64]
+    fin[0, 1] = rows[64:128]
+    send(fin.at[0, o], dev(z, y, x, o), fin_slot, fin.at[1, 0])
+    arrived(fin.at[1, 0], fin_slot)
+    for core in range(2):
+
+        @pl.when(c == core)
+        def _():
+            sent[:, 128 * core : 128 * (core + 1)] = fin[0, core]
+            sent[:, 128 * (1 - core) : 128 * (2 - core)] = fin[1, 0]
+
     for k in range(NZ):
         pltpu.make_async_copy(stage.at[k], wg.at[:, pl.ds(k * 1024, 1024)], out_sem.at[k]).wait()
     for copy in sends:
@@ -288,20 +489,26 @@
     assert count[0] <= N_SEM, count
 
 
-def forward(hidden, targets, out_weight):
+def on_device(hidden, targets, out_weight):
     hbm, vmem = pl.BlockSpec(memory_space=pl.ANY), pl.BlockSpec(memory_space=pltpu.VMEM)
-    loss, wg, dlt = pl.pallas_call(
+    heavy = [
+        pltpu.VMEM((NZ, 4, BC, 128), WIRE),
+        pltpu.VMEM((NZ, 4, BC, 128), WIRE),
+        pltpu.VMEM((NZ, 2, 4, BC, 128), WIRE),
+        pltpu.VMEM((NZ, 2, 4, BC, 128), WIRE),
+    ]
+    loss, weight_grad, sent = pl.pallas_call(
         body,
         out_shape=(
             jax.ShapeDtypeStruct((4, 128), F32),
             jax.ShapeDtypeStruct((RV, D), BF16),
-            jax.ShapeDtypeStruct((RV, T), BF16),
+            jax.ShapeDtypeStruct((64, 256), BF16),
         ),
         in_specs=[hbm, vmem, hbm],
         out_specs=(vmem, hbm, vmem),
         scratch_shapes=[
             pltpu.VMEM((2, NZ, NY, NX, NC, 64, 128), BF16),
-            pltpu.VMEM((NZ * NY, RV, 128), BF16),
+            pltpu.VMEM((NZ * NY, 2 * RV, 128), BF16),
             pltpu.VMEM((NZ * NY, RV, 128), BF16),
             pltpu.VMEM((RV, T), F32),
             pltpu.VMEM((RV, T), BF16),
@@ -309,6 +516,22 @@
             pltpu.VMEM((NC, 16, 128), F32),
             pltpu.VMEM((NX * NY, 16, 128), F32),
             pltpu.VMEM((NZ, 16, 128), F32),
+            pltpu.VMEM((T, 2 * RV), BF16),
+            pltpu.VMEM((NZ, NY, NX, 128, 128), F32),
+            *heavy,
+            *heavy,
+            pltpu.VMEM((4, NY, NX, 32, 128), WIRE),
+            pltpu.VMEM((4, NY, NX, 32, 128), WIRE),
+            pltpu.VMEM((4, NY, NX, 32, 128), WIRE),
+            pltpu.VMEM((4, NY, NX, 32, 128), WIRE),
+            pltpu.VMEM((2, 4, BC, 128), F32),
+            pltpu.VMEM((2, 2, 4, BC, 128), F32),
+            pltpu.VMEM((2, 4, BC, 128), F32),
+            pltpu.VMEM((2, 2, 4, BC, 128), F32),
+            pltpu.VMEM((NZ - 1, 96, 128), F32),
+            pltpu.VMEM((NY, NX, 32, 128), F32),
+            pltpu.VMEM((NX * NY - 1, 32, 128), F32),
+            pltpu.VMEM((2, 2, 64, 128), BF16),
             pltpu.SemaphoreType.DMA((N_SEM,)),
             pltpu.SemaphoreType.DMA((N_SEM,)),
             pltpu.SemaphoreType.DMA((2,)),
@@ -316,23 +539,10 @@
             pltpu.SemaphoreType.DMA((NZ,)),
         ],
         compiler_params=pltpu.CompilerParams(
-            collective_id=0, has_side_effects=True, vmem_limit_bytes=60 * 2**20
+            collective_id=0, has_side_effects=True, vmem_limit_bytes=62 * 2**20
         ),
     )(hidden, targets.reshape(1, T), out_weight)
-    return loss.reshape(T), wg, dlt
-
-
-def on_device(hidden, targets, out_weight):
-    token_loss, weight_grad, dlt = forward(hidden, targets, out_weight)
-    partial = lax.dot_general(
-        dlt, out_weight, (((0,), (0,)), ((), ())), preferred_element_type=F32
-    )
-    block = lax.psum_scatter(partial, "section", scatter_dimension=0, tiled=True)
-    pieces = jnp.moveaxis(block.reshape(64, NZ * NY, 256), 1, 0)
-    owned = lax.all_to_all(pieces, "vocab", split_axis=0, concat_axis=0, tiled=True).sum(axis=0)
-    n = NX * NC
-    sent = lax.ppermute(owned.astype(BF16), "section", [(k, (k - 1) % n) for k in range(n)])
-    return token_loss, weight_grad, sent
+    return loss.reshape(T), weight_grad, sent
 
 
 def solution(mesh):

time: 257 us -> 110 us (0.43)
  waiting for transfers between devices: 95.4 us -> 0 us
  blocking collectives: 57.8 us -> 0 us
  Pallas kernels: 63.4 us -> 101 us
  between operations: 14.1 us -> 0.64 us
  matrix products: 13.2 us -> 0 us
  starting transfers between devices: 3.16 us -> 0 us
    reduce_scatter x1 -> x0, waiting for transfers between devices: 93.2 us -> none  [on_device(): lax.psum_scatter(partial, 'section', scatter_dimension=0, tiled=True)]
    all_to_all x1 -> x0, blocking collectives: 57.8 us -> none  [on_device(): lax.all_to_all(pieces, 'vocab', split_axis=0, concat_axis=0, tiled=True)]
    pallas_call x1, Pallas kernels: 63.4 us -> 101 us  [on_device(): pl.pallas_call(body, out_shape=(jax.ShapeDtypeStruct((4, 128), F32), jax....]
    dot_general x1 -> x0, matrix products: 13.2 us -> none  [on_device(): lax.dot_general(dlt, out_weight, (((0,), (0,)), ((), ())), preferred_elem...]
    ppermute x1 -> x0, starting transfers between devices: 3.12 us -> none  [on_device(): lax.ppermute(owned.astype(BF16), 'section', [(k, (k - 1) % n) for k in ra...]
  transfers between devices with their start and end apart: 2 -> 0, of which waited for: 2 -> 0; matrix products, arithmetic and copies ran while one was open for 0% -> 0% of each run, Pallas kernels for 0% -> 0%
where the time goes in v2:
time: 110 us
  Pallas kernels  101 us (92%)
  local copies, waits for them, and re-layouts  8.08 us (7%)
    pallas_call x1, Pallas kernels, on_device(): pl.pallas_call(body, out_shape=(jax.ShapeDtypeStruct((4, 128), F32), jax....  101 us
    unnamed x5, local copies, waits for them, and re-layouts  8.08 us

profile of v2, /device:TPU:1, one launch (start us, length us, event | category | flops | bytes accessed | tf_op | source)
XLA Modules:
  0.0 110.0 jit_solution(15192560197521697618)
XLA Ops:
  0.6 101.3 %shard_map.58 = (f32[4,128]{1,0:T(4,128)}, bf16[384,8192]{1,0:T(8,128)(2,1)}, bf16[64,256]{1,0:T(8,128)(2,1)}) custom-call(bf16[64,256]{1,0:T(8,128)(2,1)} %hid.1, s32[1,512]{1,0:T(1,128)} %bitcast.2, bf16[384,8192]{1,0:T(8,128)(2,1)} %w.1), custom_call_target="tpu_custom_call" | custom-call | tf_op jit(solution)/shard_map/pallas_call | solution.py:500
  101.9 1.3 %copy.9 = f32[512]{0:T(512)} copy(f32[512]{0:T(512)} %bitcast.3) | data formatting | bytes 4096
  103.2 0.0 copy-start
  103.2 6.2 %copy.10 = bf16[384,8192]{1,0:T(8,128)(2,1)} copy(bf16[384,8192]{1,0:T(8,128)(2,1)} %get-tuple-element.13) | data formatting | bytes 12582912
  109.4 0.0 copy-done
  109.4 0.6 copy.11
Async XLA Ops:
  103.2 6.2 %copy-start = (bf16[64,256]{1,0:T(8,128)(2,1)S(1)}, bf16[64,256]{1,0:T(8,128)(2,1)}, u32[]{:S(2)}) copy-start(bf16[64,256]{1,0:T(8,128)(2,1)} %get-tuple-element.14) | copy-start | bytes 98308

commit v3 on v1

v3 whole, which is shorter than its diff:
```python
import jax
import jax.numpy as jnp
from jax import lax
from jax.experimental import pallas as pl
from jax.experimental.pallas import tpu as pltpu
from jax.sharding import PartitionSpec as P

NZ, NY, NX, NC = 8, 4, 4, 2
D, T, RV = 8192, 512, 384
MESH = pl.DeviceIdType.MESH
F32, BF16 = jnp.float32, jnp.bfloat16
N_SEM = 400
WIRE = BF16
B, C = slice(0, 64), slice(64, 128)
NEAR = (0, -1, 1, -2, 2, -3, 3, 4)
ORDER = (4, 3, -3, 2, -2, 1, -1, 0)


def packed(row):
    return jnp.concatenate([row[:, 128 * k : 128 * (k + 1)] for k in range(4)], axis=0)


def unpacked(block):
    return jnp.concatenate([block[k : k + 1, :] for k in range(4)], axis=1)


def body(hid, tgt, w, loss, wg, sent, gat, wv, wo, acc, acc_o, dlt, rx_c, rx_p, rx_z, dl, part,
         sb1, rb1, sb2, rb2, sc1, rc1, sc2, rc2, qs, zb, rzb, rzf, fz, rf,
         send_sem, recv_sem, load_sem, own_sem):
    v, s = lax.axis_index("vocab"), lax.axis_index("section")
    z, y, x, c = v // NY, lax.rem(v, NY), s // NC, lax.rem(s, NC)
    o = 1 - c

    def dev(z_, y_, x_, c_):
        return (z_ * NY + y_, x_ * NC + c_)

    def zz(k):
        return lax.rem(z + (k + NZ), NZ)

    def yy(k):
        return lax.rem(y + (k + NY), NY)

    def xx(k):
        return lax.rem(x + (k + NX), NX)

    def load_w(k, _):
        own = pltpu.make_async_copy(
            w.at[:, pl.ds(pl.multiple_of(k * 256 + c * 128, 128), 128)], wv.at[k, 0:RV], load_sem.at[0]
        )
        other = pltpu.make_async_copy(
            w.at[:, pl.ds(pl.multiple_of(k * 256 + o * 128, 128), 128)], wo.at[k], load_sem.at[1]
        )
        own.start()
        other.start()
        return 0

    mine = [
        pltpu.make_async_copy(
            hid.at[:, pl.ds(128 * h, 128)], gat.at[h, z, y, x, c], own_sem.at[h]
        )
        for h in range(2)
    ]
    for copy in mine:
        copy.start()
    lax.fori_loop(0, NZ * NY, load_w, 0)

    plane = [(i, j) for i in range(NX) for j in range(NY) if (i, j) != (0, 0)]
    barrier = pltpu.get_barrier_semaphore()
    pl.semaphore_signal(barrier, inc=1, device_id=dev(z, y, x, o), device_id_type=MESH)
    for i, j in plane:
        pl.semaphore_signal(barrier, inc=1, device_id=dev(z, yy(j), xx(i), c), device_id_type=MESH)
    for k in range(1, NZ):
        pl.semaphore_signal(barrier, inc=1, device_id=dev(zz(k), y, x, c), device_id_type=MESH)
    for k in range(1, 4):
        pl.semaphore_signal(barrier, inc=1, device_id=dev(z, yy(k), x, o), device_id_type=MESH)
        pl.semaphore_signal(barrier, inc=1, device_id=dev(z, y, xx(k), o), device_id_type=MESH)
    pl.semaphore_wait(barrier, 1 + len(plane) + NZ - 1 + 6)
    for copy in mine:
        copy.wait()

    count = [0]
    sends = []

    def slot():
        count[0] += 1
        return count[0] - 1

    def send(ref, device, k, to=None, at=None):
        copy = pltpu.make_async_remote_copy(
            src_ref=ref, dst_ref=ref if to is None else to,
            send_sem=send_sem.at[k], recv_sem=recv_sem.at[k if at is None else at],
            device_id=device, device_id_type=MESH,
        )
        copy.start()
        sends.append(copy)

    def arrived(ref, k):
        pltpu.make_async_remote_copy(
            src_ref=ref, dst_ref=ref, send_sem=send_sem.at[0], recv_sem=recv_sem.at[k],
            device_id=dev(z, y, x, o), device_id_type=MESH,
        ).wait_recv()

    passed = [[] for _ in range(NZ)]

    def pass_on(i, view):
        k = slot()
        send(view(c), dev(z, y, x, o), k)
        passed[i].append((view, k))

    first = [(slot(), slot()) for _ in range(3)]
    for j in range(1, 4):
        send(gat.at[0, z, y, x, c], dev(z, yy(j), x, c), first[j - 1][0])
        send(gat.at[1, z, y, x, c], dev(z, y, xx(j), c), first[j - 1][1])
    w_slot = slot()
    pltpu.make_async_copy(wv.at[:, 0:RV, :], wo, load_sem.at[1]).wait()
    send(wo, dev(z, y, x, o), w_slot, wv.at[:, RV : 2 * RV, :])

    class Ring:
        def __init__(self, q, i):
            self.q, self.i, self.z = q, i, zz(NEAR[i])
            self.k = [slot() for _ in range(4)]

        def view(self, step, lo, hi):
            if self.q == 0:
                return lambda core: gat.at[0, self.z, lo:hi, xx(step), core]
            return lambda core: gat.at[1, self.z, yy(step), lo:hi, core]

        def to(self, step):
            return dev(z, y, xx(step), c) if self.q == 0 else dev(z, yy(step), x, c)

        def open(self):
            send(self.view(0, 0, 4)(c), self.to(1), self.k[0])
            send(self.view(0, 0, 4)(c), self.to(-1), self.k[1])

        def middle(self):
            low, high = self.view(-1, 0, 4), self.view(1, 0, 4)
            arrived(low(c), self.k[0])
            send(self.view(-1, 0, 2)(c), self.to(1), self.k[2])
            pass_on(self.i, low)
            arrived(high(c), self.k[1])
            send(self.view(1, 2, 4)(c), self.to(-1), self.k[3])
            pass_on(self.i, high)

        def close(self):
            low, high = self.view(-2, 0, 2), self.view(2, 2, 4)
            arrived(low(c), self.k[2])
            pass_on(self.i, low)
            arrived(high(c), self.k[3])
            pass_on(self.i, high)

    ring = [(Ring(0, i), Ring(1, i)) for i in range(NZ)]

    def opened(*chunks):
        for i in chunks:
            ring[i][0].open()
            ring[i][1].open()

    def middle(i):
        ring[i][0].middle()
        ring[i][1].middle()

    def close(i):
        ring[i][0].close()
        ring[i][1].close()

    def unit(q, z_, lo, hi):
        if q == 0:
            return lambda core: gat.at[0, z_, lo:hi, x, core]
        return lambda core: gat.at[1, z_, y, lo:hi, core]

    near = (0, -1, 1, 2)

    def block(q, z_, m):
        if q == 0:
            return gat.at[0, z_, yy(near[m]), x, c]
        return gat.at[1, z_, y, xx(near[m]), c]

    def far(d, m):
        return (m < 2) == (d == 0)

    k_ring = {
        (d, k, m, q): slot()
        for d in range(2) for k in range(1, 5) for m in range(4) for q in range(2)
        if k < 4 or far(d, m)
    }

    def z_open(m):
        for q in range(2):
            for d in range(2):
                send(block(q, z, m), dev(zz(1 - 2 * d), y, x, c), k_ring[d, 1, m, q])

    def z_block(k, m):
        for q in range(2):
            for d in range(2):
                if k < 4 or far(d, m):
                    ref = block(q, zz(k * (2 * d - 1)), m)
                    arrived(ref, k_ring[d, k, m, q])
                    if k < 3 or (k == 3 and far(d, m)):
                        send(ref, dev(zz(1 - 2 * d), y, x, c), k_ring[d, k + 1, m, q])

    def z_done(*chunks):
        opened(*chunks)
        for i in chunks:
            for q in range(2):
                pass_on(i, unit(q, zz(NEAR[i]), 0, 4))

    def logits_step(i):
        for view, k in passed[i]:
            arrived(view(o), k)
        if i == 0:
            pltpu.make_async_copy(wo, wv.at[:, 0:RV, :], load_sem.at[0]).wait()
        zs = zz(NEAR[i])
        left, right = [], []
        for j in range(NY):
            left += [wv[zs * NY + j, 0:RV], wo[zs * NY + j]]
            right += [gat[c, zs, j].reshape(T, 128), gat[o, zs, j].reshape(T, 128)]
        res = lax.dot_general(
            jnp.concatenate(left, axis=1), jnp.concatenate(right, axis=1),
            (((1,), (1,)), ((), ())), preferred_element_type=F32,
        )
        if i == 0:
            acc[...] = res
        else:
            acc[...] += res

    def first_block(m):
        j = (0, 1, 3, 2)[m]
        arrived(gat.at[0, z, yy(-j), x, c], first[j - 1][0])
        arrived(gat.at[1, z, y, xx(-j), c], first[j - 1][1])
        z_open(m)

    z_open(0)
    first_block(1)
    first_block(2)
    z_block(1, 0)
    first_block(3)
    z_done(0)
    z_block(1, 1)
    z_block(1, 2)
    z_block(2, 0)
    z_block(1, 3)
    z_done(1, 2)
    z_block(2, 1)
    z_block(2, 2)
    z_block(3, 0)
    middle(0)
    z_block(2, 3)
    z_done(3, 4)
    z_block(3, 1)
    z_block(3, 2)
    z_block(4, 0)
    middle(1)
    z_block(3, 3)
    z_done(5, 6)
    middle(2)
    z_block(4, 1)
    z_block(4, 2)
    z_block(4, 3)
    z_done(7)
    middle(3)
    close(0)
    middle(4)
    logits_step(0)
    close(1)
    middle(5)
    close(2)
    logits_step(1)
    middle(6)
    close(3)
    logits_step(2)
    close(4)
    middle(7)
    logits_step(3)
    close(5)
    logits_step(4)
    close(6)
    logits_step(5)
    close(7)
    logits_step(6)
    logits_step(7)
    acc_slot = slot()
    send(acc, dev(z, y, x, o), acc_slot, acc_o)
    arrived(wv.at[:, RV : 2 * RV, :], w_slot)

    offset = (v * (NX * NC) + s) * RV
    picked = tgt[...] - offset == lax.broadcasted_iota(jnp.int32, (RV, T), 0)
    logits = acc[...]
    hit = jnp.sum(jnp.where(picked, logits, 0.0), axis=0, keepdims=True)
    top = jnp.max(logits, axis=0, keepdims=True)
    total = jnp.sum(jnp.exp(logits - top), axis=0, keepdims=True)
    state = jnp.concatenate([packed(top), packed(total), packed(hit), jnp.zeros((4, 128), F32)], axis=0)

    def merged(blocks):
        tops = [block[0:4] for block in blocks]
        top = tops[0]
        for one in tops[1:]:
            top = jnp.maximum(top, one)
        total, hit = jnp.zeros_like(top), jnp.zeros_like(top)
        for block, one in zip(blocks, tops):
            total = total + block[4:8] * jnp.exp(one - top)
            hit = hit + block[8:12]
        return jnp.concatenate([top, total, hit, jnp.zeros((4, 128), F32)], axis=0)

    def exchanged(state, buf, me, n, peers):
        buf[me] = state
        todo = []
        for device, source, k in peers:
            send(buf.at[me], device, k)
            todo.append((source, k))
        for source, k in todo:
            arrived(buf.at[source], k)
        return merged([buf[k] for k in range(n)])

    state = exchanged(state, rx_c, c, 2, [(dev(z, y, x, o), o, slot())])
    state = exchanged(
        state, rx_p, x * NY + y, NX * NY,
        [(dev(z, yy(j), xx(i), c), xx(-i) * NY + yy(-j), slot()) for i, j in plane],
    )
    state = exchanged(
        state, rx_z, z, NZ, [(dev(zz(k), y, x, c), zz(-k), slot()) for k in range(1, NZ)]
    )
    loss[...] = unpacked(state[0:4] + jnp.log(state[4:8]) - state[8:12])
    top, total = unpacked(state[0:4]), unpacked(state[4:8])
    dlt[...] = (jnp.exp(acc[...] - top) / total - picked.astype(F32)).astype(BF16)

    arrived(acc_o, acc_slot)
    offset_o = (v * (NX * NC) + x * NC + o) * RV
    picked_o = tgt[...] - offset_o == lax.broadcasted_iota(jnp.int32, (RV, T), 0)
    dlt_o = (jnp.exp(acc_o[...] - top) / total - picked_o.astype(F32)).astype(BF16)
    for k, value in ((0, dlt[...]), (RV, dlt_o)):
        value = jnp.transpose(value)
        dl[:, k : k + RV] = jnp.concatenate([value[64:T], value[0:64]], axis=0)

    def weight_step(k):
        right = []
        for j in range(NY):
            right += [gat[0, k, j].reshape(T, 128), gat[1, k, j].reshape(T, 128)]
        wg[:, 1024 * k : 1024 * (k + 1)] = jnp.dot(
            dlt[...], jnp.concatenate(right, axis=1), preferred_element_type=F32
        ).astype(BF16)

    def hidden_step(i):
        zd = zz(ORDER[i])
        right = jnp.concatenate([wv[zd * NY + j] for j in range(NY)], axis=1)
        res = jnp.dot(dl[...], right, preferred_element_type=F32)
        for j in range(NY):
            part[i, j] = res[:, 128 * j : 128 * (j + 1)].reshape(NX, 128, 128)

    class Heavy:
        def __init__(self, unit, along, s1, r1, s2, r2):
            self.unit, self.along = unit, along
            self.s1, self.r1, self.s2, self.r2 = s1, r1, s2, r2
            self.k = [[slot() for _ in range(4)] for _ in range(NZ)]

        def to(self, step):
            return dev(z, y, xx(step), c) if self.along == "x" else dev(z, yy(step), x, c)

        def first(self, i):
            self.s1[i] = self.unit(i, 2).astype(WIRE)
            k = self.k[i]
            send(self.s1.at[i, 0:2], self.to(1), k[0], self.r1.at[i, 0:2])
            send(self.s1.at[i, 2:4], self.to(-1), k[1], self.r1.at[i, 2:4])

        def second(self, i):
            k = self.k[i]
            for d, lo, hi in ((0, 0, 2), (1, 2, 4)):
                step = 1 - 2 * d
                arrived(self.r1.at[i, lo:hi], k[d])
                mine = self.unit(i, step)
                self.s2[i, d] = mine.astype(WIRE)
                self.s2[i, d, lo:hi] = (mine[lo:hi] + self.r1[i, lo:hi].astype(F32)).astype(WIRE)
                send(self.s2.at[i, d], self.to(step), k[2 + d], self.r2.at[i, d])

        def third(self, i):
            for d in range(2):
                arrived(self.r2.at[i, d], self.k[i][2 + d])
            return self.unit(i, 0) + self.r2[i, 0].astype(F32) + self.r2[i, 1].astype(F32)

    hb = Heavy(lambda i, step: part[i, :, xx(step), B, :], "x", sb1, rb1, sb2, rb2)
    hc = Heavy(lambda i, step: part[i, yy(step), :, C, :], "y", sc1, rc1, sc2, rc2)

    def thirds(i):
        qs[i, 0] = hb.third(i)
        qs[i, 1] = hc.third(i)

    k_z = {(d, off, h, q): slot() for d in range(2) for off in range(1, 5) for h in range(2) for q in range(2)}

    def z_send(d, off, h):
        i = ORDER.index(off if d == 0 or off == 4 else -off)
        rows = slice(2 * h, 2 * h + 2)
        for q in range(2):
            k, value = k_z[d, off, h, q], qs[i, q, rows]
            if off < 3 or (off == 3 and h == d):
                came = rzb.at[d, 3 - off] if off > 1 else rzf.at[d, 0]
                arrived(came.at[q, rows], k_z[d, off + 1, h, q])
                value = value + came[q, rows].astype(F32)
            if off > 2:
                zb[d, 4 - off, q, rows] = value.astype(WIRE)
                src, dst = zb.at[d, 4 - off, q, rows], rzb.at[d, 4 - off, q, rows]
            else:
                qs[i, q, rows] = value
                src, dst = qs.at[i, q, rows], rzf.at[d, 2 - off, q, rows]
            send(src, dev(zz(1 - 2 * d), y, x, c), k, dst)

    f_send = [[slot() for _ in range(4)] for _ in range(2)]
    f_recv = slot()
    for _ in range(7):
        slot()

    def last_send(q):
        for d in range(2):
            for h in range(2):
                arrived(rzf.at[d, 1, q, 2 * h : 2 * h + 2], k_z[d, 1, h, q])
        fz[q] = qs[NZ - 1, q] + rzf[0, 1, q] + rzf[1, 1, q]
        for j in range(1, 4):
            block = yy(j) if q == 0 else xx(j)
            device = dev(z, block, x, 0) if q == 0 else dev(z, y, block, 1)
            send(fz.at[q, block], device, f_send[q][j], rf.at[c, j], f_recv + 4 * c + j)


    def go(i):
        hidden_step(i)
        hb.first(i)
        hc.first(i)

    def second(i):
        hb.second(i)
        hc.second(i)

    go(0)
    go(1)
    go(2)
    weight_step(0)
    second(0)
    go(3)
    second(1)
    go(4)
    second(2)
    weight_step(1)
    thirds(0)
    z_send(0, 4, 0)
    z_send(1, 4, 1)
    go(5)
    second(3)
    thirds(1)
    z_send(0, 3, 1)
    go(6)
    second(4)
    weight_step(2)
    thirds(2)
    z_send(1, 3, 0)
    z_send(0, 3, 0)
    z_send(1, 3, 1)
    go(7)
    second(5)
    thirds(3)
    z_send(0, 2, 1)
    z_send(0, 2, 0)
    second(6)
    weight_step(3)
    thirds(4)
    z_send(1, 2, 0)
    z_send(1, 2, 1)
    second(7)
    weight_step(4)
    thirds(5)
    z_send(0, 1, 1)
    z_send(0, 1, 0)
    weight_step(5)
    thirds(6)
    z_send(1, 1, 0)
    z_send(1, 1, 1)
    weight_step(6)
    thirds(7)
    weight_step(7)
    last_send(0)
    last_send(1)
    mine = y * (1 - c) + x * c
    theirs = y * (1 - o) + x * o
    send(fz.at[o, theirs], dev(z, y, x, o), f_send[0][0], rf.at[c, 0], f_recv + 4 * c)
    rf[c, 0] = fz[c, mine]
    arrived(rf.at[o, 0], f_recv + 4 * o)
    for core in range(2):
        for j in range(1, 4):
            arrived(rf.at[core, j], f_recv + 4 * core + j)
    for core in range(2):
        total = rf[core, 0] + rf[core, 1] + rf[core, 2] + rf[core, 3]
        sent[:, 128 * core : 128 * (core + 1)] = total.astype(BF16)
    for copy in sends:
        copy.wait_send()
    assert count[0] <= N_SEM, count


def on_device(hidden, targets, out_weight):
    hbm, vmem = pl.BlockSpec(memory_space=pl.ANY), pl.BlockSpec(memory_space=pltpu.VMEM)
    heavy = [
        pltpu.VMEM((NZ, 4, 64, 128), WIRE),
        pltpu.VMEM((NZ, 4, 64, 128), WIRE),
        pltpu.VMEM((NZ, 2, 4, 64, 128), WIRE),
        pltpu.VMEM((NZ, 2, 4, 64, 128), WIRE),
    ]
    loss, weight_grad, sent = pl.pallas_call(
        body,
        out_shape=(
            jax.ShapeDtypeStruct((1, T), F32),
            jax.ShapeDtypeStruct((RV, D), BF16),
            jax.ShapeDtypeStruct((64, 256), BF16),
        ),
        in_specs=[hbm, vmem, hbm],
        out_specs=(vmem, vmem, vmem),
        scratch_shapes=[
            pltpu.VMEM((2, NZ, NY, NX, NC, 64, 128), BF16),
            pltpu.VMEM((NZ * NY, 2 * RV, 128), BF16),
            pltpu.VMEM((NZ * NY, RV, 128), BF16),
            pltpu.VMEM((RV, T), F32),
            pltpu.VMEM((RV, T), F32),
            pltpu.VMEM((RV, T), BF16),
            pltpu.VMEM((NC, 16, 128), F32),
            pltpu.VMEM((NX * NY, 16, 128), F32),
            pltpu.VMEM((NZ, 16, 128), F32),
            pltpu.VMEM((T, 2 * RV), BF16),
            pltpu.VMEM((NZ, NY, NX, 128, 128), F32),
            *heavy,
            *heavy,
            pltpu.VMEM((NZ, 2, 4, 64, 128), F32),
            pltpu.VMEM((2, 2, 2, 4, 64, 128), WIRE),
            pltpu.VMEM((2, 2, 2, 4, 64, 128), WIRE),
            pltpu.VMEM((2, 2, 2, 4, 64, 128), F32),
            pltpu.VMEM((2, 4, 64, 128), F32),
            pltpu.VMEM((2, 4, 64, 128), F32),
            pltpu.SemaphoreType.DMA((N_SEM,)),
            pltpu.SemaphoreType.DMA((N_SEM,)),
            pltpu.SemaphoreType.DMA((2,)),
            pltpu.SemaphoreType.DMA((2,)),
        ],
        compiler_params=pltpu.CompilerParams(
            collective_id=0, has_side_effects=True, vmem_limit_bytes=46 * 2**20
        ),
    )(hidden, targets.reshape(1, T), out_weight)
    return loss.reshape(T), weight_grad, sent


def solution(mesh):
    placed = (P("section", "vocab"), P(), P(("vocab", "section"), None))
    return jax.shard_map(
        on_device, mesh=mesh, in_specs=placed,
        out_specs=(P(), P(("vocab", "section"), None), P("section", "vocab")),
        check_vma=False,
    )
```

time: 257 us -> 98.5 us (0.38)
  waiting for transfers between devices: 95.4 us -> 0 us
  blocking collectives: 57.8 us -> 0 us
  Pallas kernels: 63.4 us -> 92.3 us
  between operations: 14.1 us -> 0.65 us
  matrix products: 13.2 us -> 0 us
  local copies, waits for them, and re-layouts: 9.21 us -> 5.33 us
  starting transfers between devices: 3.16 us -> 0 us
    reduce_scatter x1 -> x0, waiting for transfers between devices: 93.2 us -> none  [on_device(): lax.psum_scatter(partial, 'section', scatter_dimension=0, tiled=True)]
    all_to_all x1 -> x0, blocking collectives: 57.8 us -> none  [on_device(): lax.all_to_all(pieces, 'vocab', split_axis=0, concat_axis=0, tiled=True)]
    pallas_call x1, Pallas kernels: 63.4 us -> 92.3 us  [on_device(): pl.pallas_call(body, out_shape=(jax.ShapeDtypeStruct((1, T), F32), jax.Sh...]
    dot_general x1 -> x0, matrix products: 13.2 us -> none  [on_device(): lax.dot_general(dlt, out_weight, (((0,), (0,)), ((), ())), preferred_elem...]
    ppermute x1 -> x0, starting transfers between devices: 3.12 us -> none  [on_device(): lax.ppermute(owned.astype(BF16), 'section', [(k, (k - 1) % n) for k in ra...]
    unnamed x5 -> x7, local copies, waits for them, and re-layouts: 7.39 us -> 5.33 us
  transfers between devices with their start and end apart: 2 -> 0, of which waited for: 2 -> 0; matrix products, arithmetic and copies ran while one was open for 0% -> 0% of each run, Pallas kernels for 0% -> 0%
where the time goes in v3:
time: 98.5 us; the launch traced here: 98.3 us
  Pallas kernels  92.3 us (94%)
  local copies, waits for them, and re-layouts  5.33 us (5%)
    pallas_call x1, Pallas kernels, on_device(): pl.pallas_call(body, out_shape=(jax.ShapeDtypeStruct((1, T), F32), jax.Sh...  92.3 us
    unnamed x7, local copies, waits for them, and re-layouts  5.33 us

profile of v3, /device:TPU:1, one launch (start us, length us, event | category | flops | bytes accessed | tf_op | source)
XLA Modules:
  0.0 98.3 jit_solution(11014686810271280240)
XLA Ops:
  0.6 0.0 copy-start
  0.6 0.7 copy-done
  1.4 0.0 copy-start.1
  1.4 0.7 copy-done.1
  2.1 92.3 %shard_map.58 = (f32[1,512]{1,0:T(1,128)S(1)}, bf16[384,8192]{1,0:T(8,128)(2,1)S(1)}, bf16[64,256]{1,0:T(8,128)(2,1)S(1)}) custom-call(bf16[64,256]{1,0:T(8,128)(2,1)S(1)} %copy-done, s32[1,512]{1,0:T(1,128)S(1)} %bitcast.2, bf16[384,8192]{1,0:T(8,128)(2,1)} %w.1), custom_call_target="tpu_custom_call" | custom-call | tf_op jit(solution)/shard_map/pallas_call | solution.py:502
  94.4 0.6 copy.9
  95.0 2.7 %copy.10 = bf16[384,8192]{1,0:T(8,128)(2,1)} copy(bf16[384,8192]{1,0:T(8,128)(2,1)S(1)} %get-tuple-element.13) | data formatting | bytes 12582912
  97.7 0.6 copy.11
Async XLA Ops:
  0.6 0.8 copy-start
  1.4 0.7 copy-start.1
